TPU v7x, 32 devices: a whole 2x2x4 slice. The times are simulated.
32 devices in a mesh: wide: 8 (over z, x), narrow: 4 (over y, core).
Axes of the slice: x: 2, y: 2, z: 4, core: 2. Of those that a mesh axis runs over, the one named last changes fastest.
Arguments:
- tokens: bfloat16 [4096, 1024], P(('wide', 'narrow')), may hold values from -6 to 6
- cotangent: bfloat16 [4096, 1024], P(('wide', 'narrow')), may hold values from -0.0625 to 0.0625
- segment_ids: int32 [32, 128], P(('wide', 'narrow')), may hold values from 0 to 7, never falling along the last dimension, each value on 1 to 32 neighbouring positions
- w_qkv: float32 [1024, 3072], P(('wide', 'narrow')), may hold values from -0.1875 to 0.1875
- w_out: float32 [1024, 1024], P(('wide', 'narrow')), may hold values from -0.375 to 0.375
- w_up: float32 [1024, 4096], P(('wide', 'narrow')), may hold values from -0.1875 to 0.1875
- w_down: float32 [4096, 1024], P(('wide', 'narrow')), may hold values from -0.09375 to 0.09375
- vectors: float32 [1024, 12], P(('wide', 'narrow')), as said below
- moments_qkv: float32 [2, 1024, 3072], P(None, ('wide', 'narrow')), as said below
- moments_out: float32 [2, 1024, 1024], P(None, ('wide', 'narrow')), as said below
- moments_up: float32 [2, 1024, 4096], P(None, ('wide', 'narrow')), as said below
- moments_down: float32 [2, 4096, 1024], P(None, ('wide', 'narrow')), as said below
- moments_vec: float32 [2, 1024, 12], P(None, ('wide', 'narrow')), as said below
Outputs:
- block_out: bfloat16 [4096, 1024], P(('wide', 'narrow'))
- input_grad: float32 [4096, 1024], P(('wide', 'narrow'))
- new_qkv: float32 [1024, 3072], P(('wide', 'narrow'))
- new_out: float32 [1024, 1024], P(('wide', 'narrow'))
- new_up: float32 [1024, 4096], P(('wide', 'narrow'))
- new_down: float32 [4096, 1024], P(('wide', 'narrow'))
- new_vectors: float32 [1024, 12], P(('wide', 'narrow'))
- state_qkv: float32 [2, 1024, 3072], P(None, ('wide', 'narrow'))
- state_out: float32 [2, 1024, 1024], P(None, ('wide', 'narrow'))
- state_up: float32 [2, 1024, 4096], P(None, ('wide', 'narrow'))
- state_down: float32 [2, 4096, 1024], P(None, ('wide', 'narrow'))
- state_vectors: float32 [2, 1024, 12], P(None, ('wide', 'narrow'))
- copy_qkv: bfloat16 [1024, 3072], P(('wide', 'narrow'))
- copy_out: bfloat16 [1024, 1024], P(('wide', 'narrow'))
- copy_up: bfloat16 [1024, 4096], P(('wide', 'narrow'))
- copy_down: bfloat16 [4096, 1024], P(('wide', 'narrow'))
- copy_vectors: bfloat16 [1024, 12], P(('wide', 'narrow'))
Inputs may be any that keep to these rules, and one draw needn't show every extreme that they name: `segment_ids`: in each sequence the ids never fall, every id is used, each segment has 1 to 32 patches and one has exactly 32. `vectors`: columns 0 and 5 are positive gains; the others are biases of both signs. `moments_qkv`: the second slice is positive. `moments_out`: the second slice is positive. `moments_up`: the second slice is positive. `moments_down`: the second slice is positive. `moments_vec`: the second slice is positive.
All inputs are finite; a program needn't handle non-finite values.
Results may differ from a plain program's by a relative error of at most 0.02.
Values may be sent and summed in bfloat16 or wider, within the bound.
A program may use at most 256 MiB of HBM per device.

v0:
```python
import jax
import jax.numpy as jnp
from jax import lax
from jax.sharding import PartitionSpec as P

D = 1024
HEADS = 16
FF = 4096
STEP = 3
NORM_EPSILON = 1e-06
MASK_VALUE = -1e30
MOMENT_DECAY = 0.5
RATE_MATRIX = 0.04
RATE_VECTOR = 0.2
WEIGHT_DECAY = 0.1
ADAM_EPSILON = 1e-08


def layer_norm(values, scale_row, offset_row):
    center = values - jnp.mean(values, axis=-1, keepdims=True)
    spread = jnp.mean(center * center, axis=-1, keepdims=True)
    return center * lax.rsqrt(spread + NORM_EPSILON) * scale_row + offset_row


def exact_gelu(values):
    return jax.nn.gelu(values, approximate=False)


def adam_update(master, moments, gradient, rate, decay):
    first_moment = MOMENT_DECAY * moments[0] + (1.0 - MOMENT_DECAY) * gradient
    second_moment = MOMENT_DECAY * moments[1] + (1.0 - MOMENT_DECAY) * gradient * gradient
    correction = 1.0 - MOMENT_DECAY**STEP
    normalized = first_moment / correction / (jnp.sqrt(second_moment / correction) + ADAM_EPSILON)
    updated = master - rate * (normalized + decay * master)
    return (updated, jnp.stack([first_moment, second_moment]), updated.astype(jnp.bfloat16))


def unpack_vectors(packed):
    columns = [packed[:, column] for column in range(8)]
    columns.append(packed[:, 8:].T.reshape(FF))
    return columns


def body(
    tokens,
    cotangent,
    segment_ids,
    w_qkv,
    w_out,
    w_up,
    w_down,
    vectors,
    moments_qkv,
    moments_out,
    moments_up,
    moments_down,
    moments_vec,
):
    qkv_low = w_qkv.astype(jnp.bfloat16)
    out_low = w_out.astype(jnp.bfloat16)
    up_low = w_up.astype(jnp.bfloat16)
    down_low = w_down.astype(jnp.bfloat16)
    vec_low = vectors.astype(jnp.bfloat16)
    gathered = (
        lax.all_gather(qkv_low, ("wide", "narrow"), axis=0, tiled=True),
        lax.all_gather(out_low, ("wide", "narrow"), axis=0, tiled=True),
        lax.all_gather(up_low, ("wide", "narrow"), axis=0, tiled=True),
        lax.all_gather(down_low, ("wide", "narrow"), axis=0, tiled=True),
        lax.all_gather(vec_low, ("wide", "narrow"), axis=0, tiled=True),
    )
    qkv_full, out_full, up_full, down_full, vec_full = gathered
    length = tokens.shape[0]
    block_rows = min(512, length)
    block_count = length // block_rows
    head_dim = D // HEADS
    scale_value = head_dim ** (-0.5)
    segments = segment_ids[0]
    (
        gain_one,
        shift_one,
        bias_query,
        bias_value,
        bias_out,
        gain_two,
        shift_two,
        bias_down,
        bias_up,
    ) = unpack_vectors(vec_full.astype(jnp.float32))
    inputs = tokens.astype(jnp.float32)
    normed_one = layer_norm(inputs, gain_one, shift_one).astype(jnp.bfloat16)
    qkv_bias = jnp.concatenate([bias_query, jnp.zeros_like(bias_query), bias_value])
    qkv_value = (
        jnp.dot(normed_one, qkv_full, preferred_element_type=jnp.float32) + qkv_bias
    ).astype(jnp.bfloat16)
    queries = qkv_value[:, :D].reshape(length, HEADS, head_dim)
    keys_all = qkv_value[:, D : 2 * D].reshape(length, HEADS, head_dim)
    values_all = qkv_value[:, 2 * D :].reshape(length, HEADS, head_dim)
    query_blocks = queries.reshape(block_count, block_rows, HEADS, head_dim)
    segment_blocks = segments.reshape(block_count, block_rows)

    def masked_scores(query_block, segment_block):
        raw_scores = (
            jnp.einsum("qhd,khd->hqk", query_block, keys_all, preferred_element_type=jnp.float32)
            * scale_value
        )
        same_segment = segment_block[:, None] == segments[None, :]
        return jnp.where(same_segment[None], raw_scores, MASK_VALUE)

    def attend(pieces):
        query_block, segment_block = pieces
        scores = masked_scores(query_block, segment_block)
        highest = jnp.max(scores, axis=-1, keepdims=True)
        exp_scores = jnp.exp(scores - highest)
        totals = jnp.sum(exp_scores, axis=-1, keepdims=True)
        soft_weights = (exp_scores / totals).astype(jnp.bfloat16)
        mixed = jnp.einsum(
            "hqk,khd->qhd", soft_weights, values_all, preferred_element_type=jnp.float32
        )
        return (mixed.astype(jnp.bfloat16), (highest + jnp.log(totals))[:, :, 0])

    attended, log_totals = lax.map(attend, (query_blocks, segment_blocks))
    attended = attended.reshape(length, D)
    resid_one = inputs + jnp.dot(attended, out_full, preferred_element_type=jnp.float32) + bias_out
    normed_two = layer_norm(resid_one, gain_two, shift_two).astype(jnp.bfloat16)
    hidden_pre = jnp.dot(normed_two, up_full, preferred_element_type=jnp.float32) + bias_up
    hidden_act, gelu_pull = jax.vjp(exact_gelu, hidden_pre)
    hidden_low = hidden_act.astype(jnp.bfloat16)
    block_out = (
        resid_one + jnp.dot(hidden_low, down_full, preferred_element_type=jnp.float32) + bias_down
    ).astype(jnp.bfloat16)
    back_weights = (
        lax.all_gather(qkv_low, ("wide", "narrow"), axis=0, tiled=True),
        lax.all_gather(out_low, ("wide", "narrow"), axis=0, tiled=True),
        lax.all_gather(up_low, ("wide", "narrow"), axis=0, tiled=True),
        lax.all_gather(down_low, ("wide", "narrow"), axis=0, tiled=True),
        lax.all_gather(vec_low, ("wide", "narrow"), axis=0, tiled=True),
    )
    qkv_back, out_back, up_back, down_back, vec_back = back_weights
    back_params = unpack_vectors(vec_back.astype(jnp.float32))
    grad_down = jnp.einsum("sf,sd->fd", hidden_low, cotangent, preferred_element_type=jnp.float32)
    grad_bias_down = jnp.sum(cotangent.astype(jnp.float32), axis=0)
    grad_hidden = jnp.einsum("sd,fd->sf", cotangent, down_back, preferred_element_type=jnp.float32)
    grad_pre = gelu_pull(grad_hidden)[0].astype(jnp.bfloat16)
    grad_up = jnp.einsum("sd,sf->df", normed_two, grad_pre, preferred_element_type=jnp.float32)
    grad_bias_up = jnp.sum(grad_pre.astype(jnp.float32), axis=0)
    grad_normed_two = jnp.einsum("sf,df->sd", grad_pre, up_back, preferred_element_type=jnp.float32)
    norm_value_two, norm_pull_two = jax.vjp(layer_norm, resid_one, back_params[5], back_params[6])
    part_resid, grad_gain_two, grad_shift_two = norm_pull_two(grad_normed_two)
    grad_resid = cotangent.astype(jnp.float32) + part_resid
    grad_branch = grad_resid.astype(jnp.bfloat16)
    grad_out = jnp.einsum("sd,se->de", attended, grad_branch, preferred_element_type=jnp.float32)
    grad_bias_out = jnp.sum(grad_resid, axis=0)
    grad_attended = jnp.einsum(
        "se,de->sd", grad_branch, out_back, preferred_element_type=jnp.float32
    ).astype(jnp.bfloat16)
    grad_blocks = grad_attended.reshape(block_count, block_rows, HEADS, head_dim)

    def attend_back(running, pieces):
        key_grad, value_grad = running
        query_block, segment_block, grad_block, log_block = pieces
        scores = masked_scores(query_block, segment_block)
        soft_weights = jnp.exp(scores - log_block[:, :, None])
        value_grad = value_grad + jnp.einsum(
            "hqk,qhd->khd",
            soft_weights.astype(jnp.bfloat16),
            grad_block,
            preferred_element_type=jnp.float32,
        )
        grad_soft = jnp.einsum(
            "qhd,khd->hqk", grad_block, values_all, preferred_element_type=jnp.float32
        )
        inner_sum = jnp.sum(soft_weights * grad_soft, axis=-1, keepdims=True)
        grad_scores = (soft_weights * (grad_soft - inner_sum)).astype(jnp.bfloat16)
        query_grad = (
            jnp.einsum("hqk,khd->qhd", grad_scores, keys_all, preferred_element_type=jnp.float32)
            * scale_value
        )
        key_grad = (
            key_grad
            + jnp.einsum(
                "hqk,qhd->khd", grad_scores, query_block, preferred_element_type=jnp.float32
            )
            * scale_value
        )
        return ((key_grad, value_grad), query_grad)

    zero_heads = jnp.zeros((length, HEADS, head_dim), jnp.float32)
    (key_grad, value_grad), query_grad = lax.scan(
        attend_back,
        (zero_heads, zero_heads),
        (query_blocks, segment_blocks, grad_blocks, log_totals),
    )
    grad_qkv = jnp.concatenate(
        [query_grad.reshape(length, D), key_grad.reshape(length, D), value_grad.reshape(length, D)],
        axis=1,
    ).astype(jnp.bfloat16)
    grad_qkv_weight = jnp.einsum(
        "sd,sf->df", normed_one, grad_qkv, preferred_element_type=jnp.float32
    )
    qkv_sums = jnp.sum(grad_qkv.astype(jnp.float32), axis=0)
    grad_normed_one = jnp.einsum(
        "sf,df->sd", grad_qkv, qkv_back, preferred_element_type=jnp.float32
    )
    norm_value_one, norm_pull_one = jax.vjp(layer_norm, inputs, back_params[0], back_params[1])
    part_input, grad_gain_one, grad_shift_one = norm_pull_one(grad_normed_one)
    input_grad = grad_resid + part_input
    vector_head = jnp.stack(
        [
            grad_gain_one,
            grad_shift_one,
            qkv_sums[:D],
            qkv_sums[2 * D :],
            grad_bias_out,
            grad_gain_two,
            grad_shift_two,
            grad_bias_down,
        ],
        axis=1,
    )
    vector_grad = jnp.concatenate([vector_head, grad_bias_up.reshape(FF // D, D).T], axis=1)
    wide_count = lax.axis_size("wide")
    narrow_count = lax.axis_size("narrow")

    def split_rows(gradient):
        return gradient.reshape(
            wide_count,
            narrow_count,
            gradient.shape[0] // (wide_count * narrow_count),
            gradient.shape[1],
        )

    group_sums = (
        lax.psum_scatter(
            split_rows(grad_qkv_weight).astype(jnp.bfloat16),
            "narrow",
            scatter_dimension=1,
            tiled=True,
        ).astype(jnp.float32),
        lax.psum_scatter(
            split_rows(grad_out).astype(jnp.bfloat16), "narrow", scatter_dimension=1, tiled=True
        ).astype(jnp.float32),
        lax.psum_scatter(
            split_rows(grad_up).astype(jnp.bfloat16), "narrow", scatter_dimension=1, tiled=True
        ).astype(jnp.float32),
        lax.psum_scatter(
            split_rows(grad_down).astype(jnp.bfloat16), "narrow", scatter_dimension=1, tiled=True
        ).astype(jnp.float32),
        lax.psum_scatter(
            split_rows(vector_grad).astype(jnp.bfloat16), "narrow", scatter_dimension=1, tiled=True
        ).astype(jnp.float32),
    )
    owned_sums = (
        lax.psum_scatter(
            group_sums[0].astype(jnp.bfloat16), "wide", scatter_dimension=0, tiled=True
        ).astype(jnp.float32),
        lax.psum_scatter(
            group_sums[1].astype(jnp.bfloat16), "wide", scatter_dimension=0, tiled=True
        ).astype(jnp.float32),
        lax.psum_scatter(
            group_sums[2].astype(jnp.bfloat16), "wide", scatter_dimension=0, tiled=True
        ).astype(jnp.float32),
        lax.psum_scatter(
            group_sums[3].astype(jnp.bfloat16), "wide", scatter_dimension=0, tiled=True
        ).astype(jnp.float32),
        lax.psum_scatter(
            group_sums[4].astype(jnp.bfloat16), "wide", scatter_dimension=0, tiled=True
        ).astype(jnp.float32),
    )
    reduced = tuple((member.reshape(member.shape[2], member.shape[3]) for member in owned_sums))
    new_qkv, state_qkv, copy_qkv = adam_update(
        w_qkv, moments_qkv, reduced[0], RATE_MATRIX, WEIGHT_DECAY
    )
    new_out, state_out, copy_out = adam_update(
        w_out, moments_out, reduced[1], RATE_MATRIX, WEIGHT_DECAY
    )
    new_up, state_up, copy_up = adam_update(w_up, moments_up, reduced[2], RATE_MATRIX, WEIGHT_DECAY)
    new_down, state_down, copy_down = adam_update(
        w_down, moments_down, reduced[3], RATE_MATRIX, WEIGHT_DECAY
    )
    new_vectors, state_vectors, copy_vectors = adam_update(
        vectors, moments_vec, reduced[4], RATE_VECTOR, 0.0
    )
    return (
        block_out,
        input_grad,
        new_qkv,
        new_out,
        new_up,
        new_down,
        new_vectors,
        state_qkv,
        state_out,
        state_up,
        state_down,
        state_vectors,
        copy_qkv,
        copy_out,
        copy_up,
        copy_down,
        copy_vectors,
    )


def solution(mesh):
    placed = (
        P(("wide", "narrow"), None),
        P(("wide", "narrow"), None),
        P(("wide", "narrow"), None),
        P(("wide", "narrow"), None),
        P(("wide", "narrow"), None),
        P(("wide", "narrow"), None),
        P(("wide", "narrow"), None),
        P(("wide", "narrow"), None),
        P(None, ("wide", "narrow"), None),
        P(None, ("wide", "narrow"), None),
        P(None, ("wide", "narrow"), None),
        P(None, ("wide", "narrow"), None),
        P(None, ("wide", "narrow"), None),
    )
    return jax.shard_map(
        body,
        mesh=mesh,
        in_specs=placed,
        out_specs=(
            P(("wide", "narrow"), None),
            P(("wide", "narrow"), None),
            P(("wide", "narrow"), None),
            P(("wide", "narrow"), None),
            P(("wide", "narrow"), None),
            P(("wide", "narrow"), None),
            P(("wide", "narrow"), None),
            P(None, ("wide", "narrow"), None),
            P(None, ("wide", "narrow"), None),
            P(None, ("wide", "narrow"), None),
            P(None, ("wide", "narrow"), None),
            P(None, ("wide", "narrow"), None),
            P(("wide", "narrow"), None),
            P(("wide", "narrow"), None),
            P(("wide", "narrow"), None),
            P(("wide", "narrow"), None),
            P(("wide", "narrow"), None),
        ),
        check_vma=False,
    )
```

profile of v0, /device:TPU:0, one launch (start us, length us, event | category | flops | bytes accessed | tf_op | source)
XLA Modules:
  0.0 1126.8 jit_solution(3805992562656520872)
XLA Ops:
  7.3 1.8 convert_element_type.142
  9.1 1.5 convert_element_type.147
  10.7 1.8 convert_element_type.149
  12.6 0.7 convert_element_type.151
  13.6 43.8 %all-gather = bf16[32,32,12]{1,2,0:T(8,128)(2,1)S(1)} all-gather(bf16[1,32,12]{1,2,0:T(8,128)(2,1)S(1)} %convert_bitcast_fusion.10), channel_id=1, replica_groups=mesh['wide'=8,'narrow'=4] {'wide','narrow'}, dimensions={0}, use_global_device_ids=true | all-gather | bytes 25344 | tf_op jit(solution)/shard_map/all_gather | solution.py:69
  58.1 25.6 %all-gather.6.cloned.1.call-done = bf16[1024,3072]{1,0:T(8,128)(2,1)} async-done(((bf16[32,3072]{1,0:T(8,128)(2,1)}), bf16[1024,3072]{1,0:T(8,128)(2,1)}) %all-gather.6.cloned.1.call-update) | async-done | bytes 6291472 | tf_op jit(solution)/shard_map/all_gather | solution.py:65
  83.7 3.9 fusion
  89.1 52.9 %all-gather.8.cloned.1.call-done = bf16[1024,1024]{1,0:T(8,128)(2,1)} async-done(((bf16[32,1024]{1,0:T(8,128)(2,1)}), bf16[1024,1024]{1,0:T(8,128)(2,1)}) %all-gather.8.cloned.1.call-update) | async-done | bytes 2097168 | tf_op jit(solution)/shard_map/all_gather | solution.py:66
  141.9 2.1 fusion.110
  144.3 77.0 %all-gather.10.cloned.1.call-done = bf16[1024,4096]{1,0:T(8,128)(2,1)} async-done(((bf16[32,4096]{1,0:T(8,128)(2,1)}), bf16[1024,4096]{1,0:T(8,128)(2,1)}) %all-gather.10.cloned.1.call-update) | async-done | bytes 8388624 | tf_op jit(solution)/shard_map/all_gather | solution.py:67
  221.3 6.1 convolution_add_fusion
  227.4 72.9 %all-gather.12.cloned.1.call-done = bf16[4096,1024]{1,0:T(8,128)(2,1)} async-done(((bf16[128,1024]{1,0:T(8,128)(2,1)}), bf16[4096,1024]{1,0:T(8,128)(2,1)}) %all-gather.12.cloned.1.call-update) | async-done | bytes 8388624 | tf_op jit(solution)/shard_map/all_gather | solution.py:68
  300.3 10.9 fusion.102
  311.2 3.0 multiply_reduce_fusion.1
  314.5 0.8 convolution_convert_fusion.5
  316.0 1.3 multiply_reduce_fusion
  318.9 4.7 convolution_convert_fusion.2
  323.6 5.7 convolution_convert_fusion.1
  329.8 5.1 fusion.91
  335.2 1.1 fusion.90
  337.9 5.6 convolution_convert_fusion
  343.4 2.1 convolution_convert_fusion.3
  346.8 9.2 reduce-scatter.27.cloned.1.call-done
  356.0 1.4 copy.96
  357.4 424.2 %all-reduce.7.cloned.1.call-done = (bf16[8,4,32,3072]{3,2,1,0:T(8,128)(2,1)}, bf16[8,4,32,1024]{3,2,1,0:T(8,128)(2,1)}, bf16[8,4,32,4096]{3,2,1,0:T(8,128)(2,1)}, bf16[8,4,128,1024]{3,2,1,0:T(8,128)(2,1)}) async-done(((bf16[8,4,32,3072]{3,2,1,0:T(8,128)(2,1)}, bf16[8,4,32,1024]{3,2,1,0:T(8,128)(2,1)}, bf16[8,4,32,4096]{3,2,1,0:T(8,128)(2,1)}, bf16[8,4,128,1024]{3,2,1,0:T(8,128)(2,1)}), ...) | async-done | bytes 25165840
  781.6 2.5 constant_dynamic-slice_fusion.2
  784.2 3.3 constant_dynamic-slice_fusion.3
  787.6 3.8 constant_dynamic-slice_fusion.1
  792.1 5.4 fusion.10
  797.5 3.8 constant_dynamic-slice_fusion
  801.3 39.0 %reduce-scatter.29.cloned.1.call-done = bf16[1,1,32,12]{2,3,1,0:T(8,128)(2,1)} async-done(((bf16[8,1,32,12]{2,3,1,0:T(8,128)(2,1)}), bf16[1,1,32,12]{2,3,1,0:T(8,128)(2,1)}) %reduce-scatter.29.cloned.1.call-update) | async-done | bytes 784 | tf_op jit(solution)/shard_map/reduce_scatter | solution.py:265
  841.6 1.3 fusion.92
  842.9 63.0 %reduce-scatter.21.cloned.1.call-done = bf16[1,1,32,1024]{3,2,1,0:T(8,128)(2,1)} async-done(((bf16[8,1,32,1024]{3,2,1,0:T(8,128)(2,1)}), bf16[1,1,32,1024]{3,2,1,0:T(8,128)(2,1)}) %reduce-scatter.21.cloned.1.call-update) | async-done | bytes 65552 | tf_op jit(solution)/shard_map/reduce_scatter | solution.py:256
  905.9 0.9 multiply_add_fusion.6
  906.7 0.7 pad_maximum_fusion.4
  907.5 1.7 fusion.98
  909.2 64.7 %reduce-scatter.19.cloned.1.call-done = bf16[1,1,32,3072]{3,2,1,0:T(8,128)(2,1)} async-done(((bf16[8,1,32,3072]{3,2,1,0:T(8,128)(2,1)}), bf16[1,1,32,3072]{3,2,1,0:T(8,128)(2,1)}) %reduce-scatter.19.cloned.1.call-update) | async-done | bytes 196624 | tf_op jit(solution)/shard_map/reduce_scatter | solution.py:253
  973.8 1.1 multiply_add_fusion.4
  975.0 0.9 pad_maximum_fusion.3
  975.9 1.1 fusion.100
  977.0 67.6 %reduce-scatter.23.cloned.1.call-done = bf16[1,1,32,4096]{3,2,1,0:T(8,128)(2,1)} async-done(((bf16[8,1,32,4096]{3,2,1,0:T(8,128)(2,1)}), bf16[1,1,32,4096]{3,2,1,0:T(8,128)(2,1)}) %reduce-scatter.23.cloned.1.call-update) | async-done | bytes 262160 | tf_op jit(solution)/shard_map/reduce_scatter | solution.py:259
  1044.6 1.1 multiply_add_fusion.1
  1045.7 1.0 pad_maximum_fusion
  1046.7 68.8 %reduce-scatter.25.cloned.1.call-done = bf16[1,1,128,1024]{3,2,1,0:T(8,128)(2,1)} async-done(((bf16[8,1,128,1024]{3,2,1,0:T(8,128)(2,1)}), bf16[1,1,128,1024]{3,2,1,0:T(8,128)(2,1)}) %reduce-scatter.25.cloned.1.call-update) | async-done | bytes 262160 | tf_op jit(solution)/shard_map/reduce_scatter | solution.py:262
  1115.5 1.1 multiply_add_fusion
  1116.6 1.1 pad_maximum_fusion.1
  1117.7 1.3 fusion.96
  1119.0 1.3 fusion.94
  (144 shorter events, 10.9 us)
Async XLA Ops:
  7.2 5.4 copy-start.13
  7.2 6.2 copy-start.4
  7.2 6.4 copy-start.25
  7.2 50.4 %copy-start.1 = (bf16[128,1024]{1,0:T(8,128)(2,1)S(1)}, bf16[128,1024]{1,0:T(8,128)(2,1)}, u32[]{:S(2)}) copy-start(bf16[128,1024]{1,0:T(8,128)(2,1)} %param.13) | copy-start | bytes 786436
  7.2 76.4 %all-gather.6.cloned.1.call-start = ((), (), s32[]{:S(2)}) async-start(), calls=%async_computation.6 | async-start | bytes 6488064 | tf_op jit(solution)/shard_map/all_gather | solution.py:65
  9.0 48.9 %copy-start.27 = (s32[1,128]{1,0:T(1,128)S(1)}, s32[1,128]{1,0:T(1,128)}, u32[]{:S(2)}) copy-start(s32[1,128]{1,0:T(1,128)} %param.15) | copy-start | bytes 1540
  9.1 132.8 %all-gather.8.cloned.1.call-start = ((), (), s32[]{:S(2)}) async-start(), calls=%async_computation.7 | async-start | bytes 2162688 | tf_op jit(solution)/shard_map/all_gather | solution.py:66
  10.7 210.6 %all-gather.10.cloned.1.call-start = ((), (), s32[]{:S(2)}) async-start(), calls=%async_computation.8 | async-start | bytes 8650752 | tf_op jit(solution)/shard_map/all_gather | solution.py:67
  12.5 287.8 %all-gather.12.cloned.1.call-start = ((), (), s32[]{:S(2)}) async-start(), calls=%async_computation.9 | async-start | bytes 8650752 | tf_op jit(solution)/shard_map/all_gather | solution.py:68
  13.4 342.6 %reduce-scatter.27.cloned.1.call-start = ((), (), s32[]{:S(2)}) async-start(), calls=%async_computation.14 | async-start | bytes 122880 | tf_op jit(solution)/shard_map/reduce_scatter | solution.py:248
  87.8 1.2 copy-start.10
  88.2 0.9 copy-start.19
  89.0 138.3 %copy-start.21 = (bf16[16,64,128]{2,1,0:T(8,128)(2,1)}, bf16[16,64,128]{2,1,0:T(8,128)(2,1)S(1)}, u32[]{:S(2)}) copy-start(bf16[16,64,128]{2,1,0:T(8,128)(2,1)S(1)} %convolution_convert_fusion.6) | copy-start | bytes 786436
  300.3 10.9 copy-start
  311.2 3.0 copy-start.5
  311.2 3.3 copy-start.3
  317.4 1.0 copy-start.11
  318.9 4.7 copy-start.6
  323.6 5.7 copy-start.2
  323.6 5.7 copy-start.15
  337.6 5.9 copy-start.22
  337.6 444.0 %all-reduce.7.cloned.1.call-start = ((), (), s32[]{:S(2)}) async-start(), calls=%async_computation.16 | async-start | bytes 50331648
  345.6 0.7 copy-start.28
  345.6 494.7 %reduce-scatter.29.cloned.1.call-start = ((), (), s32[]{:S(2)}) async-start(), calls=%async_computation.15 | async-start | bytes 36864 | tf_op jit(solution)/shard_map/reduce_scatter | solution.py:265
  357.4 548.5 %reduce-scatter.21.cloned.1.call-start = ((), (), s32[]{:S(2)}) async-start(), calls=%async_computation.11 | async-start | bytes 589824 | tf_op jit(solution)/shard_map/reduce_scatter | solution.py:256
  784.1 189.7 %reduce-scatter.19.cloned.1.call-start = ((), (), s32[]{:S(2)}) async-start(), calls=%async_computation.10 | async-start | bytes 1769472 | tf_op jit(solution)/shard_map/reduce_scatter | solution.py:253
  787.5 257.1 %reduce-scatter.23.cloned.1.call-start = ((), (), s32[]{:S(2)}) async-start(), calls=%async_computation.12 | async-start | bytes 2359296 | tf_op jit(solution)/shard_map/reduce_scatter | solution.py:259
  791.4 0.7 copy-start.26
  791.4 324.1 %reduce-scatter.25.cloned.1.call-start = ((), (), s32[]{:S(2)}) async-start(), calls=%async_computation.13 | async-start | bytes 2359296 | tf_op jit(solution)/shard_map/reduce_scatter | solution.py:262
  801.2 104.6 %copy-start.20 = (f32[2,32,1024]{2,1,0:T(8,128)S(1)}, f32[2,32,1024]{2,1,0:T(8,128)}, u32[]{:S(2)}) copy-start(f32[2,32,1024]{2,1,0:T(8,128)} %param.22) | copy-start | bytes 786436
  801.2 106.3 %copy-start.24 = (f32[32,1024]{1,0:T(8,128)S(1)}, f32[32,1024]{1,0:T(8,128)}, u32[]{:S(2)}) copy-start(f32[32,1024]{1,0:T(8,128)} %param.17) | copy-start | bytes 393220
  801.2 172.6 %copy-start.9 = (f32[2,32,3072]{2,1,0:T(8,128)S(1)}, f32[2,32,3072]{2,1,0:T(8,128)}, u32[]{:S(2)}) copy-start(f32[2,32,3072]{2,1,0:T(8,128)} %param.21) | copy-start | bytes 2359300
  907.5 68.4 %copy-start.16 = (f32[32,3072]{1,0:T(8,128)S(1)}, f32[32,3072]{1,0:T(8,128)}, u32[]{:S(2)}) copy-start(f32[32,3072]{1,0:T(8,128)} %param.16) | copy-start | bytes 1179652
  973.8 2.0 copy-start.23
  974.9 69.7 %copy-start.7 = (f32[2,32,4096]{2,1,0:T(8,128)S(1)}, f32[2,32,4096]{2,1,0:T(8,128)}, u32[]{:S(2)}) copy-start(f32[2,32,4096]{2,1,0:T(8,128)} %param.23) | copy-start | bytes 3145732
  977.0 138.5 %copy-start.8 = (f32[2,128,1024]{2,1,0:T(8,128)S(1)}, f32[2,128,1024]{2,1,0:T(8,128)}, u32[]{:S(2)}) copy-start(f32[2,128,1024]{2,1,0:T(8,128)} %param.24) | copy-start | bytes 3145732
  1046.7 71.0 %copy-start.12 = (f32[32,4096]{1,0:T(8,128)S(1)}, f32[32,4096]{1,0:T(8,128)}, u32[]{:S(2)}) copy-start(f32[32,4096]{1,0:T(8,128)} %param.18) | copy-start | bytes 1572868
  1046.7 71.0 %copy-start.17 = (bf16[1,1,32,4096]{3,2,1,0:T(8,128)(2,1)S(1)}, bf16[1,1,32,4096]{3,2,1,0:T(8,128)(2,1)}, u32[]{:S(2)}) copy-start(bf16[1,1,32,4096]{3,2,1,0:T(8,128)(2,1)} %reduce-scatter.23.cloned.1.call-done) | copy-start | bytes 786436
  1116.6 2.4 copy-start.14
  1116.6 2.4 copy-start.18
Sparse Core Ops, SparseCore 0:
  11.5 72.1 all-gather.5
  87.1 54.7 all-gather.7
  145.4 75.9 all-gather.9
  224.6 75.6 all-gather.11
  337.7 18.2 reduce-scatter.26
  358.6 422.9 all-reduce.6
  785.3 54.9 reduce-scatter.28
  844.2 61.6 reduce-scatter.20
  909.3 64.4 reduce-scatter.18
  977.2 67.3 reduce-scatter.22
  1048.1 67.3 reduce-scatter.24
where the time goes:
time: 1130 us
  waiting for transfers between devices  965 us (85%)
  matrix products  58.5 us (5%)
  blocking collectives  43.8 us (4%)
  other arithmetic  24.5 us (2%)
  local copies, waits for them, and re-layouts  19.9 us (2%)
  between operations  14.4 us (1%)
    unnamed x12, waiting for transfers between devices  424 us
    all_gather x1, waiting for transfers between devices, body(): lax.all_gather(up_low, ('wide', 'narrow'), axis=0, tiled=True)  77 us
    all_gather x1, waiting for transfers between devices, body(): lax.all_gather(down_low, ('wide', 'narrow'), axis=0, tiled=True)  72.9 us
    reduce_scatter x1, waiting for transfers between devices, body(): lax.psum_scatter(group_sums[3].astype(jnp.bfloat16), 'wide', scatter_dime...  68.8 us
    reduce_scatter x1, waiting for transfers between devices, body(): lax.psum_scatter(group_sums[2].astype(jnp.bfloat16), 'wide', scatter_dime...  67.6 us
    reduce_scatter x1, waiting for transfers between devices, body(): lax.psum_scatter(group_sums[0].astype(jnp.bfloat16), 'wide', scatter_dime...  64.7 us
    reduce_scatter x1, waiting for transfers between devices, body(): lax.psum_scatter(group_sums[1].astype(jnp.bfloat16), 'wide', scatter_dime...  63 us
    all_gather x1, waiting for transfers between devices, body(): lax.all_gather(out_low, ('wide', 'narrow'), axis=0, tiled=True)  52.9 us
  transfers between devices with their start and end apart: 11, of which 11 were waited for; matrix products, arithmetic and copies ran while one was open for 5% of the time, Pallas kernels for 0%

commit v1 on v0

--- a/solution.py
+++ b/solution.py
@@ -1,3 +1,4 @@
+import functools
 import jax
 import jax.numpy as jnp
 from jax import lax
@@ -14,6 +15,14 @@
 RATE_VECTOR = 0.2
 WEIGHT_DECAY = 0.1
 ADAM_EPSILON = 1e-08
+
+
+def lots_all_scan(here_x, group_axis, dim_no):
+    e_next = tuple((here_x for _ in range(jax.lax.axis_size(group_axis))))
+    return jnp.concatenate(jax.lax.all_to_all(jnp.stack(e_next), group_axis, 0, 0), axis=dim_no)
+
+
+wait_the_scenes = functools.partial(lots_all_scan, group_axis=("wide", "narrow"), dim_no=0)
 
 
 def layer_norm(values, scale_row, offset_row):
@@ -64,7 +73,7 @@
     gathered = (
         lax.all_gather(qkv_low, ("wide", "narrow"), axis=0, tiled=True),
         lax.all_gather(out_low, ("wide", "narrow"), axis=0, tiled=True),
-        lax.all_gather(up_low, ("wide", "narrow"), axis=0, tiled=True),
+        wait_the_scenes(up_low),
         lax.all_gather(down_low, ("wide", "narrow"), axis=0, tiled=True),
         lax.all_gather(vec_low, ("wide", "narrow"), axis=0, tiled=True),
     )

time: 1130 us -> 1210 us (1.071)
  blocking collectives: 43.8 us -> 204 us
  waiting for transfers between devices: 965 us -> 877 us
    all_gather x1, blocking collectives: 43.8 us -> 204 us  [body(): lax.all_gather(vec_low, ('wide', 'narrow'), axis=0, tiled=True)]
    all_gather x1, waiting for transfers between devices: 52.9 us -> 0.7 us  [body(): lax.all_gather(out_low, ('wide', 'narrow'), axis=0, tiled=True)]
    all_gather x1, waiting for transfers between devices: 25.6 us -> 0.02 us  [body(): lax.all_gather(qkv_low, ('wide', 'narrow'), axis=0, tiled=True)]
  transfers between devices with their start and end apart: 11 -> 12, of which waited for: 11 -> 11; matrix products, arithmetic and copies ran while one was open for 5% -> 6% of each run, Pallas kernels for 0% -> 0%
where the time goes in v1:
time: 1210 us
  waiting for transfers between devices  877 us (72%)
  blocking collectives  204 us (17%)
  matrix products  62.4 us (5%)
  local copies, waits for them, and re-layouts  24.2 us (2%)
  other arithmetic  23.8 us (2%)
  between operations  14.4 us (1%)
    unnamed x12, waiting for transfers between devices  425 us
    all_gather x1, blocking collectives, body(): lax.all_gather(vec_low, ('wide', 'narrow'), axis=0, tiled=True)  204 us
    reduce_scatter x1, waiting for transfers between devices, body(): lax.psum_scatter(group_sums[3].astype(jnp.bfloat16), 'wide', scatter_dime...  69 us
    all_gather x1, waiting for transfers between devices, body(): lax.all_gather(up_low, ('wide', 'narrow'), axis=0, tiled=True)  68.2 us
    reduce_scatter x1, waiting for transfers between devices, body(): lax.psum_scatter(group_sums[2].astype(jnp.bfloat16), 'wide', scatter_dime...  67.4 us
    reduce_scatter x1, waiting for transfers between devices, body(): lax.psum_scatter(group_sums[0].astype(jnp.bfloat16), 'wide', scatter_dime...  64.9 us
    reduce_scatter x1, waiting for transfers between devices, body(): lax.psum_scatter(group_sums[1].astype(jnp.bfloat16), 'wide', scatter_dime...  63 us
    all_gather x1, waiting for transfers between devices, body(): lax.all_gather(down_low, ('wide', 'narrow'), axis=0, tiled=True)  62.5 us
  transfers between devices with their start and end apart: 12, of which 11 were waited for; matrix products, arithmetic and copies ran while one was open for 6% of the time, Pallas kernels for 0%

profile of v1, /device:TPU:0, one launch (start us, length us, event | category | flops | bytes accessed | tf_op | source)
XLA Modules:
  0.0 1213.8 jit_solution(9089258670706939455)
XLA Ops:
  7.2 1.7 convert_element_type.142
  9.1 1.5 convert_element_type.147
  10.7 1.8 convert_element_type.151
  12.5 4.3 stack.12
  16.8 7.5 all-to-all-start
  25.1 204.2 %all-gather = bf16[32,32,12]{1,2,0:T(8,128)(2,1)S(1)} all-gather(bf16[1,32,12]{1,2,0:T(8,128)(2,1)S(1)} %convert_bitcast_fusion.10), channel_id=1, replica_groups=mesh['wide'=8,'narrow'=4] {'wide','narrow'}, dimensions={0}, use_global_device_ids=true | all-gather | bytes 25344 | tf_op jit(solution)/shard_map/all_gather | solution.py:78
  230.0 3.9 fusion
  236.1 2.1 fusion.110
  238.5 7.9 all-to-all-done
  246.4 6.1 convolution_add_fusion
  252.5 62.5 %all-gather.10.cloned.1.call-done = bf16[4096,1024]{1,0:T(8,128)(2,1)} async-done(((bf16[128,1024]{1,0:T(8,128)(2,1)}), bf16[4096,1024]{1,0:T(8,128)(2,1)}) %all-gather.10.cloned.1.call-update) | async-done | bytes 8388624 | tf_op jit(solution)/shard_map/all_gather | solution.py:77
  315.0 10.8 fusion.102
  325.8 68.2 %all-gather.12.cloned.1.call-done = bf16[1024,4096]{1,0:T(8,128)(2,1)} async-done(((bf16[32,4096]{1,0:T(8,128)(2,1)}), bf16[1024,4096]{1,0:T(8,128)(2,1)}) %all-gather.12.cloned.1.call-update) | async-done | bytes 8388624 | tf_op jit(solution)/shard_map/all_gather | solution.py:143
  394.0 6.9 multiply_reduce_fusion.1
  401.2 0.8 convolution_convert_fusion.5
  402.7 1.3 multiply_reduce_fusion
  405.6 4.7 convolution_convert_fusion.2
  410.2 5.7 convolution_convert_fusion.1
  416.4 5.1 fusion.91
  421.9 1.1 fusion.90
  424.5 5.6 convolution_convert_fusion
  430.1 2.1 convolution_convert_fusion.3
  433.4 9.2 reduce-scatter.27.cloned.1.call-done
  442.7 1.4 copy.96
  444.1 424.2 %all-reduce.7.cloned.1.call-done = (bf16[8,4,32,3072]{3,2,1,0:T(8,128)(2,1)}, bf16[8,4,32,1024]{3,2,1,0:T(8,128)(2,1)}, bf16[8,4,32,4096]{3,2,1,0:T(8,128)(2,1)}, bf16[8,4,128,1024]{3,2,1,0:T(8,128)(2,1)}) async-done(((bf16[8,4,32,3072]{3,2,1,0:T(8,128)(2,1)}, bf16[8,4,32,1024]{3,2,1,0:T(8,128)(2,1)}, bf16[8,4,32,4096]{3,2,1,0:T(8,128)(2,1)}, bf16[8,4,128,1024]{3,2,1,0:T(8,128)(2,1)}), ...) | async-done | bytes 25165840
  868.2 2.5 constant_dynamic-slice_fusion.2
  870.8 3.3 constant_dynamic-slice_fusion.3
  874.2 3.8 constant_dynamic-slice_fusion.1
  878.8 5.4 fusion.10
  884.1 3.8 constant_dynamic-slice_fusion
  887.9 39.0 %reduce-scatter.29.cloned.1.call-done = bf16[1,1,32,12]{2,3,1,0:T(8,128)(2,1)} async-done(((bf16[8,1,32,12]{2,3,1,0:T(8,128)(2,1)}), bf16[1,1,32,12]{2,3,1,0:T(8,128)(2,1)}) %reduce-scatter.29.cloned.1.call-update) | async-done | bytes 784 | tf_op jit(solution)/shard_map/reduce_scatter | solution.py:274
  928.2 1.3 fusion.92
  929.5 63.0 %reduce-scatter.21.cloned.1.call-done = bf16[1,1,32,1024]{3,2,1,0:T(8,128)(2,1)} async-done(((bf16[8,1,32,1024]{3,2,1,0:T(8,128)(2,1)}), bf16[1,1,32,1024]{3,2,1,0:T(8,128)(2,1)}) %reduce-scatter.21.cloned.1.call-update) | async-done | bytes 65552 | tf_op jit(solution)/shard_map/reduce_scatter | solution.py:265
  992.5 0.9 multiply_add_fusion.6
  993.4 0.7 pad_maximum_fusion.4
  994.1 1.7 fusion.98
  995.8 64.9 %reduce-scatter.19.cloned.1.call-done = bf16[1,1,32,3072]{3,2,1,0:T(8,128)(2,1)} async-done(((bf16[8,1,32,3072]{3,2,1,0:T(8,128)(2,1)}), bf16[1,1,32,3072]{3,2,1,0:T(8,128)(2,1)}) %reduce-scatter.19.cloned.1.call-update) | async-done | bytes 196624 | tf_op jit(solution)/shard_map/reduce_scatter | solution.py:262
  1060.7 1.1 multiply_add_fusion.4
  1061.9 0.9 pad_maximum_fusion.3
  1062.8 1.1 fusion.100
  1063.9 67.4 %reduce-scatter.23.cloned.1.call-done = bf16[1,1,32,4096]{3,2,1,0:T(8,128)(2,1)} async-done(((bf16[8,1,32,4096]{3,2,1,0:T(8,128)(2,1)}), bf16[1,1,32,4096]{3,2,1,0:T(8,128)(2,1)}) %reduce-scatter.23.cloned.1.call-update) | async-done | bytes 262160 | tf_op jit(solution)/shard_map/reduce_scatter | solution.py:268
  1131.3 1.1 multiply_add_fusion.1
  1132.4 1.0 pad_maximum_fusion
  1133.5 69.0 %reduce-scatter.25.cloned.1.call-done = bf16[1,1,128,1024]{3,2,1,0:T(8,128)(2,1)} async-done(((bf16[8,1,128,1024]{3,2,1,0:T(8,128)(2,1)}), bf16[1,1,128,1024]{3,2,1,0:T(8,128)(2,1)}) %reduce-scatter.25.cloned.1.call-update) | async-done | bytes 262160 | tf_op jit(solution)/shard_map/reduce_scatter | solution.py:271
  1202.5 1.1 multiply_add_fusion
  1203.6 1.1 pad_maximum_fusion.1
  1204.7 1.3 fusion.96
  1206.0 1.3 fusion.94
  (145 shorter events, 12.2 us)
Async XLA Ops:
  7.2 5.3 copy-start.11
  7.2 222.8 %all-gather.6.cloned.1.call-start = ((), (), s32[]{:S(2)}) async-start(), calls=%async_computation.7 | async-start | bytes 6488064 | tf_op jit(solution)/shard_map/all_gather | solution.py:74
  9.0 227.1 %all-gather.8.cloned.1.call-start = ((), (), s32[]{:S(2)}) async-start(), calls=%async_computation.8 | async-start | bytes 2162688 | tf_op jit(solution)/shard_map/all_gather | solution.py:75
  10.6 304.3 %all-gather.10.cloned.1.call-start = ((), (), s32[]{:S(2)}) async-start(), calls=%async_computation.9 | async-start | bytes 8650752 | tf_op jit(solution)/shard_map/all_gather | solution.py:77
  12.5 4.3 copy-start.8
  16.8 8.1 copy-start.3
  16.8 8.3 copy-start.24
  16.8 212.7 %copy-start = (bf16[128,1024]{1,0:T(8,128)(2,1)S(1)}, bf16[128,1024]{1,0:T(8,128)(2,1)}, u32[]{:S(2)}) copy-start(bf16[128,1024]{1,0:T(8,128)(2,1)} %param.13) | copy-start | bytes 786436
  16.8 213.0 %copy-start.26 = (s32[1,128]{1,0:T(1,128)S(1)}, s32[1,128]{1,0:T(1,128)}, u32[]{:S(2)}) copy-start(s32[1,128]{1,0:T(1,128)} %param.15) | copy-start | bytes 1540
  16.8 229.5 %all-to-all-start = ((bf16[32,32,4096]{2,1,0:T(8,128)(2,1)}), bf16[32,32,4096]{2,1,0:T(8,128)(2,1)}, u32[]{:S(2)}, u32[]{:S(2)}) async-start(bf16[32,32,4096]{2,1,0:T(8,128)(2,1)} %stack.12), calls=%async_computation | async-start | bytes 16777216 | tf_op jit(solution)/shard_map/all_to_all | solution.py:22
  24.3 369.7 %all-gather.12.cloned.1.call-start = ((), (), s32[]{:S(2)}) async-start(), calls=%async_computation.10 | async-start | bytes 8650752 | tf_op jit(solution)/shard_map/all_gather | solution.py:143
  24.9 417.8 %reduce-scatter.27.cloned.1.call-start = ((), (), s32[]{:S(2)}) async-start(), calls=%async_computation.15 | async-start | bytes 122880 | tf_op jit(solution)/shard_map/reduce_scatter | solution.py:257
  234.1 1.2 copy-start.9
  234.5 0.9 copy-start.18
  235.4 17.1 %copy-start.20 = (bf16[16,64,128]{2,1,0:T(8,128)(2,1)}, bf16[16,64,128]{2,1,0:T(8,128)(2,1)S(1)}, u32[]{:S(2)}) copy-start(bf16[16,64,128]{2,1,0:T(8,128)(2,1)S(1)} %convolution_convert_fusion.6) | copy-start | bytes 786436
  394.0 7.2 copy-start.2
  404.0 1.0 copy-start.10
  405.5 4.7 copy-start.4
  410.2 5.7 copy-start.1
  410.2 5.7 copy-start.14
  424.2 5.9 copy-start.21
  424.2 444.0 %all-reduce.7.cloned.1.call-start = ((), (), s32[]{:S(2)}) async-start(), calls=%async_computation.17 | async-start | bytes 50331648
  432.2 0.7 copy-start.27
  432.2 494.7 %reduce-scatter.29.cloned.1.call-start = ((), (), s32[]{:S(2)}) async-start(), calls=%async_computation.16 | async-start | bytes 36864 | tf_op jit(solution)/shard_map/reduce_scatter | solution.py:274
  444.0 548.5 %reduce-scatter.21.cloned.1.call-start = ((), (), s32[]{:S(2)}) async-start(), calls=%async_computation.12 | async-start | bytes 589824 | tf_op jit(solution)/shard_map/reduce_scatter | solution.py:265
  870.8 190.0 %reduce-scatter.19.cloned.1.call-start = ((), (), s32[]{:S(2)}) async-start(), calls=%async_computation.11 | async-start | bytes 1769472 | tf_op jit(solution)/shard_map/reduce_scatter | solution.py:262
  874.2 257.2 %reduce-scatter.23.cloned.1.call-start = ((), (), s32[]{:S(2)}) async-start(), calls=%async_computation.13 | async-start | bytes 2359296 | tf_op jit(solution)/shard_map/reduce_scatter | solution.py:268
  878.0 0.7 copy-start.25
  878.1 324.4 %reduce-scatter.25.cloned.1.call-start = ((), (), s32[]{:S(2)}) async-start(), calls=%async_computation.14 | async-start | bytes 2359296 | tf_op jit(solution)/shard_map/reduce_scatter | solution.py:271
  887.9 104.7 %copy-start.19 = (f32[2,32,1024]{2,1,0:T(8,128)S(1)}, f32[2,32,1024]{2,1,0:T(8,128)}, u32[]{:S(2)}) copy-start(f32[2,32,1024]{2,1,0:T(8,128)} %param.22) | copy-start | bytes 786436
  887.9 106.3 %copy-start.23 = (f32[32,1024]{1,0:T(8,128)S(1)}, f32[32,1024]{1,0:T(8,128)}, u32[]{:S(2)}) copy-start(f32[32,1024]{1,0:T(8,128)} %param.17) | copy-start | bytes 393220
  887.9 172.9 %copy-start.7 = (f32[2,32,3072]{2,1,0:T(8,128)S(1)}, f32[2,32,3072]{2,1,0:T(8,128)}, u32[]{:S(2)}) copy-start(f32[2,32,3072]{2,1,0:T(8,128)} %param.21) | copy-start | bytes 2359300
  994.1 68.7 %copy-start.15 = (f32[32,3072]{1,0:T(8,128)S(1)}, f32[32,3072]{1,0:T(8,128)}, u32[]{:S(2)}) copy-start(f32[32,3072]{1,0:T(8,128)} %param.16) | copy-start | bytes 1179652
  1060.7 2.0 copy-start.22
  1061.8 69.5 %copy-start.5 = (f32[2,32,4096]{2,1,0:T(8,128)S(1)}, f32[2,32,4096]{2,1,0:T(8,128)}, u32[]{:S(2)}) copy-start(f32[2,32,4096]{2,1,0:T(8,128)} %param.23) | copy-start | bytes 3145732
  1063.9 138.5 %copy-start.6 = (f32[2,128,1024]{2,1,0:T(8,128)S(1)}, f32[2,128,1024]{2,1,0:T(8,128)}, u32[]{:S(2)}) copy-start(f32[2,128,1024]{2,1,0:T(8,128)} %param.24) | copy-start | bytes 3145732
  1133.5 71.2 %copy-start.12 = (f32[32,4096]{1,0:T(8,128)S(1)}, f32[32,4096]{1,0:T(8,128)}, u32[]{:S(2)}) copy-start(f32[32,4096]{1,0:T(8,128)} %param.18) | copy-start | bytes 1572868
  1133.5 71.2 %copy-start.16 = (bf16[1,1,32,4096]{3,2,1,0:T(8,128)(2,1)S(1)}, bf16[1,1,32,4096]{3,2,1,0:T(8,128)(2,1)}, u32[]{:S(2)}) copy-start(bf16[1,1,32,4096]{3,2,1,0:T(8,128)(2,1)} %reduce-scatter.23.cloned.1.call-done) | copy-start | bytes 786436
  1203.6 2.4 copy-start.13
  1203.6 2.4 copy-start.17
Sparse Core Ops, SparseCore 0:
  11.5 135.1 all-gather.5
  150.1 85.9 all-gather.7
  239.5 75.4 all-gather.9
  318.3 75.6 all-gather.11
  424.3 18.2 reduce-scatter.26
  445.3 422.9 all-reduce.6
  871.9 54.9 reduce-scatter.28
  930.8 61.6 reduce-scatter.20
  995.9 64.7 reduce-scatter.18
  1064.1 67.1 reduce-scatter.22
  1134.9 67.5 reduce-scatter.24
